TPU v7x, 512 devices: a whole 4x4x16 slice. The times are simulated.
512 devices in a mesh: grp: 64 (over y, z_hi, x, core), node: 8 (over z_lo).
Axes of the slice: x: 4, y: 4, z: 16 (z_hi: 2, z_lo: 8; z = z_hi * 8 + z_lo), core: 2. Of those that a mesh axis runs over, the one named last changes fastest.
Arguments:
- grad_out: bfloat16 [24576, 2048], P('grp', 'node'), may hold values from -32 to 32
- gate_prob: float32 [24576], P('grp'), may hold values from 0.05 to 1
- hidden: bfloat16 [24576, 7168], P('grp', 'node'), may hold values from -0.19921875 to 0.19921875
- w_down: bfloat16 [2048, 7168], P(None, 'node'), may hold values from -0.0625 to 0.0625
- slot_counts: int32 [64], P('grp'), may hold values from 0 to 384, as said below
Outputs:
- grad_hidden: bfloat16 [24576, 7168], P('grp', 'node')
- grad_weight: bfloat16 [2048, 7168], P('grp', 'node')
Inputs may be any that keep to these rules, and one draw needn't show every extreme that they name: `slot_counts`: each count is a multiple of 128; in every draw some group's count is 384.
All inputs are finite; a program needn't handle non-finite values.
Results may differ from a plain program's by a relative error of at most 0.0057.
Values may be sent and summed in bfloat16 or wider, within the bound.
No kernel may reach another device: no remote copies, remote signals or barrier semaphores. Data moves between devices by JAX's collectives and lax.ppermute only.
A program may use at most 64 MiB of HBM per device.

v0:
```python
import jax
import jax.numpy as jnp
from jax import lax
from jax.sharding import PartitionSpec as P

TILE_ROWS = 128


def hidden_grads(features, w_down, tile_rows, first_tile, tile_count):
    buffer_rows = features.shape[0]
    zeros_out = jnp.zeros((buffer_rows, w_down.shape[1]), jnp.bfloat16)

    def hidden_one_tile(tile_index, result):
        tile_block = lax.dynamic_slice_in_dim(features, tile_index * tile_rows, tile_rows, 0)
        product = jnp.dot(tile_block, w_down, preferred_element_type=jnp.float32).astype(
            jnp.bfloat16
        )
        return lax.dynamic_update_slice_in_dim(result, product, tile_index * tile_rows, 0)

    return lax.fori_loop(first_tile, first_tile + tile_count, hidden_one_tile, zeros_out)


def weight_term(features, hidden_part, tile_rows, tile_count):

    def weight_one_tile(tile_index, running):
        slot_block = lax.dynamic_slice_in_dim(features, tile_index * tile_rows, tile_rows, 0)
        unit_block = lax.dynamic_slice_in_dim(hidden_part, tile_index * tile_rows, tile_rows, 0)
        return running + lax.dot_general(
            slot_block, unit_block, (((0,), (0,)), ((), ())), preferred_element_type=jnp.float32
        )

    start_sum = jnp.zeros((features.shape[1], hidden_part.shape[1]), jnp.float32)
    return lax.fori_loop(0, tile_count, weight_one_tile, start_sum)


def owner_rows(received):
    return jnp.sum(received.astype(jnp.float32), axis=0)


def body(grad_out, gate_prob, hidden, w_down, slot_counts):
    tile_rows = TILE_ROWS
    own_tiles = slot_counts[0] // tile_rows
    scaled = (gate_prob[:, None] * grad_out.astype(jnp.float32)).astype(jnp.bfloat16)
    gathered = lax.all_gather(scaled, "node", axis=1, tiled=True)
    grad_hidden = hidden_grads(gathered, w_down, tile_rows, 0, own_tiles)
    group_count = lax.axis_size("grp")
    model_rows = gathered.shape[1]
    rows_here = model_rows // group_count
    whole_term = weight_term(gathered, hidden, tile_rows, own_tiles).astype(jnp.bfloat16)
    blocks = whole_term.reshape(group_count, rows_here, hidden.shape[1])
    received = lax.all_to_all(blocks, "grp", split_axis=0, concat_axis=0, tiled=True)
    summed = owner_rows(received)
    return (grad_hidden, summed.astype(jnp.bfloat16))


def solution(mesh):
    return jax.shard_map(
        body,
        mesh=mesh,
        in_specs=(P("grp", "node"), P("grp"), P("grp", "node"), P(None, "node"), P("grp")),
        out_specs=(P("grp", "node"), P("grp", "node")),
        check_vma=False,
    )
```

profile of v0, /device:TPU:97, one launch (start us, length us, event | category | flops | bytes accessed | tf_op | source)
XLA Modules:
  0.0 307.5 jit_solution(12469548475492476656)
XLA Ops:
  7.2 0.0 all-gather.2.cloned.1.call-start
  7.2 1.7 multiply_convert_fusion
  8.9 0.0 all-gather.2.cloned.1.call-update
  9.6 61.6 %all-gather.2.cloned.1.call-done = bf16[384,2048]{1,0:T(8,128)(2,1)} async-done(((bf16[384,256]{1,0:T(8,128)(2,1)}), bf16[384,2048]{1,0:T(8,128)(2,1)}) %all-gather.2.cloned.1.call-update) | async-done | bytes 1572880 | tf_op jit(solution)/shard_map/all_gather | solution.py:44
  71.2 0.0 copy-start
  71.2 3.4 %broadcast_in_dim.8 = f32[2048,896]{1,0:T(8,128)} broadcast(f32[]{:T(128)} %constant.38.clone.1), dimensions={} | broadcast | bytes 7340036 | tf_op jit(solution)/shard_map/broadcast_in_dim | solution.py:32
  74.6 0.0 copy-done
  74.6 7.3 %while.21 = (s32[]{:T(128)}, f32[2048,896]{1,0:T(8,128)}, s32[]{:T(128)}, bf16[384,2048]{1,0:T(8,128)(2,1)S(1)}, bf16[384,896]{1,0:T(8,128)(2,1)}, /*index=5*/s32[]{:T(128)}, s32[]{:T(128)}, s32[]{:T(128)}, s32[]{:T(128)}) while((s32[]{:T(128)}, f32[2048,896]{1,0:T(8,128)}, s32[]{:T(128)}, bf16[384,2048]{1,0:T(8,128)(2,1)S(1)}, ...), condition=%wide.region_3.4_spmd, body=%wide.region_2.3_spmd.sunk | while | flops 471597056 | bytes 15434891 | solution.py:33
  74.7 7.3 %convolution_add_fusion.2 = f32[2048,896]{1,0:T(8,128)} fusion(f32[2048,896]{1,0:T(8,128)} %get-tuple-element.181, bf16[384,2048]{1,0:T(8,128)(2,1)S(1)} %get-tuple-element.192, s32[]{:T(128)S(6)} %select_n.17, bf16[384,896]{1,0:T(8,128)(2,1)} %get-tuple-element.193), kind=kOutput, calls=%fused_computation.4.clone.1 | convolution fusion | flops 471597056 | bytes 15434752 | tf_op jit(solution)/shard_map/while/body/dot_general | solution.py:28
  82.0 5.4 %convert_element_type.16 = bf16[2048,896]{1,0:T(8,128)(2,1)} convert(f32[2048,896]{1,0:T(8,128)} %get-tuple-element.59) | non-fusion elementwise | flops 1835008 | bytes 11010048 | tf_op jit(solution)/shard_map/convert_element_type | solution.py:49
  87.4 30.0 %all-to-all-start = ((bf16[64,32,896]{2,1,0:T(8,128)(2,1)}), bf16[64,32,896]{2,1,0:T(8,128)(2,1)}, u32[]{:S(2)}, u32[]{:S(2)}) async-start(bf16[64,32,896]{2,1,0:T(8,128)(2,1)} %bitcast.9), calls=%async_computation | async-start | bytes 7340032 | tf_op jit(solution)/shard_map/all_to_all | solution.py:51
  117.4 0.1 broadcast_in_dim.7
  117.4 2.8 while.20
  117.5 2.8 fusion.14
  120.2 0.0 copy-start.1
  120.3 177.2 %all-to-all-done = bf16[64,32,896]{2,1,0:T(8,128)(2,1)} async-done(((bf16[64,32,896]{2,1,0:T(8,128)(2,1)}), bf16[64,32,896]{2,1,0:T(8,128)(2,1)}, u32[]{:S(2)}, u32[]{:S(2)}) %all-to-all-start) | async-done | bytes 3670048 | tf_op jit(solution)/shard_map/all_to_all | solution.py:51
  297.4 3.2 %reduce_sum.12 = bf16[32,896]{1,0:T(8,128)(2,1)} reduce(bf16[64,32,896]{2,1,0:T(8,128)(2,1)} %all-to-all-done, bf16[]{:T(256)} %constant.33.clone.1), dimensions={0}, to_apply=%region_4.5 | reduce | flops 1806336 | bytes 3727362 | tf_op jit(solution)/shard_map/reduce_sum | solution.py:37
  300.6 0.0 copy-done.1
Async XLA Ops:
  7.2 64.1 %all-gather.2.cloned.1.call-start = ((), (), s32[]{:S(2)}) async-start(), calls=%async_computation.1 | async-start | bytes 1769472 | tf_op jit(solution)/shard_map/all_gather | solution.py:44
  71.2 3.4 %copy-start = (bf16[384,2048]{1,0:T(8,128)(2,1)S(1)}, bf16[384,2048]{1,0:T(8,128)(2,1)}, u32[]{:S(2)}) copy-start(bf16[384,2048]{1,0:T(8,128)(2,1)} %all-gather.2.cloned.1.call-done) | copy-start | bytes 4718596
  87.4 210.1 %all-to-all-start = ((bf16[64,32,896]{2,1,0:T(8,128)(2,1)}), bf16[64,32,896]{2,1,0:T(8,128)(2,1)}, u32[]{:S(2)}, u32[]{:S(2)}) async-start(bf16[64,32,896]{2,1,0:T(8,128)(2,1)} %bitcast.9), calls=%async_computation | async-start | bytes 7340032 | tf_op jit(solution)/shard_map/all_to_all | solution.py:51
  120.2 180.4 %copy-start.1 = (bf16[384,896]{1,0:T(8,128)(2,1)}, bf16[384,896]{1,0:T(8,128)(2,1)S(1)}, u32[]{:S(2)}) copy-start(bf16[384,896]{1,0:T(8,128)(2,1)S(1)} %get-tuple-element.56) | copy-start | bytes 2064388
Sparse Core Ops, SparseCore 0:
  10.6 60.6 all-gather.1
where the time goes:
time: 308 us; the launch traced here: 307 us
  waiting for transfers between devices  239 us (78%)
  starting transfers between devices  30 us (10%)
  between operations  14.7 us (5%)
  other arithmetic  10.3 us (3%)
  matrix products  10.1 us (3%)
  local copies, waits for them, and re-layouts  3.49 us (1%)
    all_to_all x1, waiting for transfers between devices, body(): lax.all_to_all(blocks, 'grp', split_axis=0, concat_axis=0, tiled=True)  177 us
    all_gather x1, waiting for transfers between devices, body(): gathered = lax.all_gather(scaled, 'node', axis=1, tiled=True)  61.6 us
    all_to_all x1, starting transfers between devices, body(): lax.all_to_all(blocks, 'grp', split_axis=0, concat_axis=0, tiled=True)  30 us
    dot_general x1, matrix products, weight_one_tile(): lax.dot_general(slot_block, unit_block, (((0,), (0,)), ((), ())), preferr...  7.32 us
  transfers between devices with their start and end apart: 2, of which 2 were waited for; matrix products, arithmetic and copies ran while one was open for 1% of the time, Pallas kernels for 0%

commit v1 on v0

--- a/solution.py
+++ b/solution.py
@@ -41,7 +41,7 @@
     tile_rows = TILE_ROWS
     own_tiles = slot_counts[0] // tile_rows
     scaled = (gate_prob[:, None] * grad_out.astype(jnp.float32)).astype(jnp.bfloat16)
-    gathered = lax.all_gather(scaled, "node", axis=1, tiled=True)
+    gathered = jnp.concatenate(lax.all_gather(scaled, "node"), axis=1)
     grad_hidden = hidden_grads(gathered, w_down, tile_rows, 0, own_tiles)
     group_count = lax.axis_size("grp")
     model_rows = gathered.shape[1]

time: 308 us -> 308 us (level)
  the two profiles are of different devices: /device:TPU:97 before, /device:TPU:103 now
where the time goes in v1:
time: 308 us
  waiting for transfers between devices  227 us (74%)
  matrix products  30.2 us (10%)
  starting transfers between devices  20.2 us (7%)
  between operations  14.7 us (5%)
  other arithmetic  10.3 us (3%)
  local copies, waits for them, and re-layouts  5.08 us (2%)
    all_to_all x1, waiting for transfers between devices, body(): lax.all_to_all(blocks, 'grp', split_axis=0, concat_axis=0, tiled=True)  171 us
    all_gather x1, waiting for transfers between devices, body(): gathered = jnp.concatenate(lax.all_gather(scaled, 'node'), axis=1)  55.9 us
    dot_general x3, matrix products, weight_one_tile(): lax.dot_general(slot_block, unit_block, (((0,), (0,)), ((), ())), preferr...  21.9 us
    all_to_all x1, starting transfers between devices, body(): lax.all_to_all(blocks, 'grp', split_axis=0, concat_axis=0, tiled=True)  20.1 us
    dot_general x3, matrix products, hidden_one_tile(): jnp.dot(tile_block, w_down, preferred_element_type=jnp.float32)  8.32 us
  transfers between devices with their start and end apart: 2, of which 2 were waited for; matrix products, arithmetic and copies ran while one was open for 3% of the time, Pallas kernels for 0%

profile of v1, /device:TPU:103, one launch (start us, length us, event | category | flops | bytes accessed | tf_op | source)
XLA Modules:
  0.0 307.6 jit_solution(6094530446661680583)
XLA Ops:
  7.2 0.0 all-gather.3.cloned.1.call-start
  7.2 1.7 multiply_convert_fusion
  8.9 0.0 all-gather.3.cloned.1.call-update
  9.6 55.9 %all-gather.3.cloned.1.call-done = bf16[3072,256]{1,0:T(8,128)(2,1)} async-done(((bf16[384,256]{1,0:T(8,128)(2,1)}), bf16[3072,256]{1,0:T(8,128)(2,1)}) %all-gather.3.cloned.1.call-update) | async-done | bytes 1572880 | tf_op jit(solution)/shard_map/all_gather | solution.py:44
  65.5 1.6 copy.8
  67.1 3.4 %broadcast_in_dim.8 = f32[2048,896]{1,0:T(8,128)} broadcast(f32[]{:T(128)} %constant.38.clone.1), dimensions={} | broadcast | bytes 7340036 | tf_op jit(solution)/shard_map/broadcast_in_dim | solution.py:32
  70.6 21.9 %while.21 = (s32[]{:T(128)}, f32[2048,896]{1,0:T(8,128)}, s32[]{:T(128)}, bf16[384,2048]{1,0:T(8,128)(2,1)S(1)}, bf16[384,896]{1,0:T(8,128)(2,1)}, /*index=5*/s32[]{:T(128)}, s32[]{:T(128)}, s32[]{:T(128)}, s32[]{:T(128)}) while((s32[]{:T(128)}, f32[2048,896]{1,0:T(8,128)}, s32[]{:T(128)}, bf16[384,2048]{1,0:T(8,128)(2,1)S(1)}, ...), condition=%wide.region_3.4_spmd, body=%wide.region_2.3_spmd.sunk | while | flops 471597056 | bytes 15434891 | solution.py:33
  70.6 7.3 %convolution_add_fusion.2 = f32[2048,896]{1,0:T(8,128)} fusion(f32[2048,896]{1,0:T(8,128)} %get-tuple-element.181, bf16[384,2048]{1,0:T(8,128)(2,1)S(1)} %get-tuple-element.192, s32[]{:T(128)S(6)} %select_n.17, bf16[384,896]{1,0:T(8,128)(2,1)} %get-tuple-element.193), kind=kOutput, calls=%fused_computation.4.clone.1 | convolution fusion | flops 471597056 | bytes 15434752 | tf_op jit(solution)/shard_map/while/body/dot_general | solution.py:28
  77.9 7.3 %convolution_add_fusion.2 = f32[2048,896]{1,0:T(8,128)} fusion(f32[2048,896]{1,0:T(8,128)} %get-tuple-element.181, bf16[384,2048]{1,0:T(8,128)(2,1)S(1)} %get-tuple-element.192, s32[]{:T(128)S(6)} %select_n.17, bf16[384,896]{1,0:T(8,128)(2,1)} %get-tuple-element.193), kind=kOutput, calls=%fused_computation.4.clone.1 | convolution fusion | flops 471597056 | bytes 15434752 | tf_op jit(solution)/shard_map/while/body/dot_general | solution.py:28
  85.2 7.3 %convolution_add_fusion.2 = f32[2048,896]{1,0:T(8,128)} fusion(f32[2048,896]{1,0:T(8,128)} %get-tuple-element.181, bf16[384,2048]{1,0:T(8,128)(2,1)S(1)} %get-tuple-element.192, s32[]{:T(128)S(6)} %select_n.17, bf16[384,896]{1,0:T(8,128)(2,1)} %get-tuple-element.193), kind=kOutput, calls=%fused_computation.4.clone.1 | convolution fusion | flops 471597056 | bytes 15434752 | tf_op jit(solution)/shard_map/while/body/dot_general | solution.py:28
  92.5 5.4 %convert_element_type.16 = bf16[2048,896]{1,0:T(8,128)(2,1)} convert(f32[2048,896]{1,0:T(8,128)} %get-tuple-element.59) | non-fusion elementwise | flops 1835008 | bytes 11010048 | tf_op jit(solution)/shard_map/convert_element_type | solution.py:49
  97.8 20.1 %all-to-all-start = ((bf16[64,32,896]{2,1,0:T(8,128)(2,1)}), bf16[64,32,896]{2,1,0:T(8,128)(2,1)}, u32[]{:S(2)}, u32[]{:S(2)}) async-start(bf16[64,32,896]{2,1,0:T(8,128)(2,1)} %bitcast.16), calls=%async_computation | async-start | bytes 7340032 | tf_op jit(solution)/shard_map/all_to_all | solution.py:51
  118.0 0.1 broadcast_in_dim.7
  118.1 8.4 %while.20 = (s32[]{:T(128)}, bf16[384,896]{1,0:T(8,128)(2,1)S(1)}, s32[]{:T(128)}, bf16[384,2048]{1,0:T(8,128)(2,1)S(1)}, bf16[2048,896]{1,0:T(8,128)(2,1)}, /*index=5*/s32[]{:T(128)}, s32[]{:T(128)}, s32[]{:T(128)}, s32[]{:T(128)}) while((s32[]{:T(128)}, bf16[384,896]{1,0:T(8,128)(2,1)S(1)}, s32[]{:T(128)}, bf16[384,2048]{1,0:T(8,128)(2,1)S(1)}, ...), condition=%wide.region_1.2_spmd, body=%wide.region_0.1_spmd.sunk | while | flops 469876736 | bytes 4424843 | solution.py:20
  118.1 2.8 fusion.14
  120.9 2.8 fusion.14
  123.7 2.8 fusion.14
  126.5 0.0 copy-start
  126.5 171.0 %all-to-all-done = bf16[64,32,896]{2,1,0:T(8,128)(2,1)} async-done(((bf16[64,32,896]{2,1,0:T(8,128)(2,1)}), bf16[64,32,896]{2,1,0:T(8,128)(2,1)}, u32[]{:S(2)}, u32[]{:S(2)}) %all-to-all-start) | async-done | bytes 3670048 | tf_op jit(solution)/shard_map/all_to_all | solution.py:51
  297.5 3.2 %reduce_sum.12 = bf16[32,896]{1,0:T(8,128)(2,1)} reduce(bf16[64,32,896]{2,1,0:T(8,128)(2,1)} %all-to-all-done, bf16[]{:T(256)} %constant.33.clone.1), dimensions={0}, to_apply=%region_4.5 | reduce | flops 1806336 | bytes 3727362 | tf_op jit(solution)/shard_map/reduce_sum | solution.py:37
  300.7 0.0 copy-done
Async XLA Ops:
  7.2 58.4 %all-gather.3.cloned.1.call-start = ((), (), s32[]{:S(2)}) async-start(), calls=%async_computation.1 | async-start | bytes 1769472 | tf_op jit(solution)/shard_map/all_gather | solution.py:44
  97.8 199.7 %all-to-all-start = ((bf16[64,32,896]{2,1,0:T(8,128)(2,1)}), bf16[64,32,896]{2,1,0:T(8,128)(2,1)}, u32[]{:S(2)}, u32[]{:S(2)}) async-start(bf16[64,32,896]{2,1,0:T(8,128)(2,1)} %bitcast.16), calls=%async_computation | async-start | bytes 7340032 | tf_op jit(solution)/shard_map/all_to_all | solution.py:51
  126.5 174.2 %copy-start = (bf16[384,896]{1,0:T(8,128)(2,1)}, bf16[384,896]{1,0:T(8,128)(2,1)S(1)}, u32[]{:S(2)}) copy-start(bf16[384,896]{1,0:T(8,128)(2,1)S(1)} %get-tuple-element.56) | copy-start | bytes 2064388
Sparse Core Ops, SparseCore 0:
  10.6 54.8 all-gather.2
